TPU v7x, 32 devices: a whole 2x2x4 slice. The times are simulated.
32 devices in a mesh: gx: 2 (over x), gy: 4 (over z), gz: 4 (over y, core).
Axes of the slice: x: 2, y: 2, z: 4, core: 2. Of those that a mesh axis runs over, the one named last changes fastest.
Arguments:
- pair_list: int32 [1024, 2], P(('gx', 'gy', 'gz')), may hold values from 0 to 63, all different within a row; in each aligned block of 32 rows (0 to 31, 32 to 63, ...) at most 2 rows name the same one
- rank_bucket: int32 [1024], P(('gx', 'gy', 'gz')), may hold values from 0 to 2
- amplitudes: bfloat16 [1024, 36864], P(('gx', 'gy', 'gz')), may hold values from -0.4375 to 0.4375
- intersects: bfloat16 [1024, 36864], P(('gx', 'gy', 'gz')), may hold values from -0.4375 to 0.4375
- integrals: bfloat16 [1024, 36864], P(('gx', 'gy', 'gz')), may hold values from -6 to 6
- exchange_blocks: bfloat16 [64, 36864], P(('gx', 'gy')), may hold values from -0.4375 to 0.4375
Outputs:
- residuals: bfloat16 [1024, 36864], P(('gx', 'gy', 'gz'))
Inputs may be any that keep to these rules, and one draw needn't show every extreme that they name: `pair_list`: each row names two different occupied orbitals; within the rows of one device no orbital is named more than 2 times, a bound that some block reaches on some devices. `rank_bucket`: bucket b keeps the leading (b + 1) * 64 PNOs.
All inputs are finite; a program needn't handle non-finite values.
Results may differ from a plain program's by a relative error of at most 0.013.
Values may be sent and summed in bfloat16 or wider, within the bound.
A program may use at most 128 MiB of HBM per device.

v0:
```python
import jax
import jax.numpy as jnp
from jax import lax
from jax.sharding import PartitionSpec as P

RSTEP = 64
R = 192


def body(pair_list, rank_bucket, amplitudes, intersects, integrals, exchange_blocks):
    pair_rows = amplitudes.shape[0]
    rank_width = R
    owned_rows = exchange_blocks.shape[0]
    amplitudes = amplitudes.reshape(pair_rows, rank_width, rank_width)
    intersects = intersects.reshape(pair_rows, rank_width, rank_width)
    integrals = integrals.reshape(pair_rows, rank_width, rank_width)
    exchange_blocks = exchange_blocks.reshape(owned_rows, rank_width, rank_width)
    groups_x, groups_y = (lax.axis_size("gx"), lax.axis_size("gy"))
    group_total = groups_x * groups_y
    occupied = owned_rows * group_total
    row_index = lax.broadcasted_iota(jnp.int32, (rank_width, rank_width), 0)
    col_index = lax.broadcasted_iota(jnp.int32, (rank_width, rank_width), 1)
    pair_rank = (rank_bucket + 1) * RSTEP
    inside = (row_index[None] < pair_rank[:, None, None]) & (
        col_index[None] < pair_rank[:, None, None]
    )
    masked = jnp.where(inside, amplitudes, jnp.zeros_like(amplitudes))
    half_projected = jnp.einsum(
        "pab,pbc->pac", intersects, masked, preferred_element_type=jnp.float32
    ).astype(jnp.bfloat16)
    projected = jnp.einsum(
        "pab,pcb->pac", half_projected, intersects, preferred_element_type=jnp.float32
    ).astype(jnp.bfloat16)
    local_term = jnp.einsum("pab,pbc->pac", masked, integrals, preferred_element_type=jnp.float32)
    flat_projected = projected.reshape(pair_rows, rank_width * rank_width)
    end_counts = jnp.sum(
        (pair_list[None] == lax.broadcasted_iota(jnp.int32, (occupied, 1, 1), 0)).astype(jnp.int32),
        axis=2,
    ).astype(jnp.bfloat16)
    partial_sum = lax.psum_scatter(
        jnp.dot(end_counts, flat_projected, preferred_element_type=jnp.float32),
        ("gx", "gy"),
        scatter_dimension=0,
        tiled=True,
    ).reshape(owned_rows, rank_width, rank_width)
    domain = lax.psum(partial_sum, "gz")
    coupled = jnp.einsum(
        "oab,obc->oac",
        domain.astype(jnp.bfloat16),
        exchange_blocks,
        preferred_element_type=jnp.float32,
    ).astype(jnp.bfloat16)
    every_coupled, every_block = (
        lax.all_gather(coupled, ("gx", "gy"), axis=0, tiled=True),
        lax.all_gather(exchange_blocks, ("gx", "gy"), axis=0, tiled=True),
    )
    picked_blocks = every_block[pair_list]
    picked_coupled = every_coupled[pair_list]
    own_term = jnp.einsum(
        "pab,pebc->peac", projected, picked_blocks, preferred_element_type=jnp.float32
    ).astype(jnp.bfloat16)
    answers = (picked_coupled.astype(jnp.float32) - own_term.astype(jnp.float32)).astype(
        jnp.bfloat16
    )
    combined = (answers[:, 0].astype(jnp.float32) + answers[:, 1].astype(jnp.float32)).astype(
        jnp.bfloat16
    )
    half_back = jnp.einsum(
        "pba,pbc->pac", intersects, combined, preferred_element_type=jnp.float32
    ).astype(jnp.bfloat16)
    back_projected = jnp.einsum(
        "pab,pbc->pac", half_back, intersects, preferred_element_type=jnp.float32
    )
    residual_sum = integrals.astype(jnp.float32) + local_term + back_projected
    result = jnp.where(inside, residual_sum, jnp.zeros_like(residual_sum)).astype(jnp.bfloat16)
    return result.reshape(pair_rows, rank_width * rank_width)


def solution(mesh):
    placed = (
        P(("gx", "gy", "gz"), None),
        P(("gx", "gy", "gz")),
        P(("gx", "gy", "gz"), None),
        P(("gx", "gy", "gz"), None),
        P(("gx", "gy", "gz"), None),
        P(("gx", "gy"), None),
    )
    return jax.shard_map(
        body, mesh=mesh, in_specs=placed, out_specs=P(("gx", "gy", "gz"), None), check_vma=False
    )
```

profile of v0, /device:TPU:0, one launch (start us, length us, event | category | flops | bytes accessed | tf_op | source)
XLA Modules:
  0.0 454.9 jit_solution(4188154951140406437)
XLA Ops:
  6.5 0.0 reduce-scatter.2.cloned.1.call-start
  6.5 6.1 %reshape.28 = bf16[32,192,192]{2,1,0:T(8,128)(2,1)} reshape(bf16[32,36864]{1,0:T(8,128)(2,1)} %param.8) | data formatting | bytes 4718592 | tf_op jit(solution)/shard_map/reshape | solution.py:14
  12.7 0.0 copy-start.1
  12.7 5.0 %reshape.29 = bf16[32,192,192]{2,1,0:T(8,128)(2,1)S(1)} reshape(bf16[32,36864]{1,0:T(8,128)(2,1)} %param.9) | data formatting | bytes 4718592 | tf_op jit(solution)/shard_map/reshape | solution.py:15
  17.6 0.0 copy-done.1
  17.7 6.9 %fusion.19 = bf16[32,192,192]{2,1,0:T(8,128)(2,1)} fusion(bf16[32,192,192]{2,1,0:T(8,128)(2,1)S(1)} %reshape.29, bf16[32,192,192]{2,1,0:T(8,128)(2,1)} %reshape.28, s32[32]{0:T(128)S(1)} %add_multiply_fusion), kind=kOutput, calls=%fused_computation.20 | convolution fusion | flops 913047552 | bytes 7078016 | tf_op jit(solution)/shard_map/pab,pcb->pac/dot_general | solution.py:31
  24.5 0.0 copy-start
  24.5 6.2 %reshape.30 = bf16[32,36864]{1,0:T(8,128)(2,1)} reshape(bf16[32,192,192]{2,1,0:T(8,128)(2,1)} %fusion.19) | data formatting | bytes 4718592 | tf_op jit(solution)/shard_map/reshape | solution.py:35
  30.7 0.0 copy-done
  30.7 0.1 convert_reduce_fusion
  30.8 6.7 %fusion.26 = f32[64,36864]{1,0:T(8,128)} fusion(bf16[32,36864]{1,0:T(8,128)(2,1)} %reshape.30, s32[64,32]{0,1:T(8,128)S(1)} %convert_reduce_fusion), kind=kOutput, calls=%fused_computation.25 | convolution fusion | flops 150996992 | bytes 11804672 | tf_op jit(solution)/shard_map/dot_general | solution.py:41
  37.5 0.0 reduce-scatter.2.cloned.1.call-update
  37.5 0.0 all-gather.5.cloned.1.call-start
  37.5 2.9 reshape.32
  40.4 0.0 all-gather.5.cloned.1.call-update
  40.5 0.0 all-gather.3.cloned.1.call-start
  40.5 162.0 %reduce-scatter.2.cloned.1.call-done = f32[8,36864]{1,0:T(8,128)} async-done(((f32[64,36864]{1,0:T(8,128)}), f32[8,36864]{1,0:T(8,128)}) %reduce-scatter.2.cloned.1.call-update) | async-done | bytes 1179664 | tf_op jit(solution)/shard_map/reduce_scatter | solution.py:40
  202.5 3.1 reshape.31
  205.6 34.0 %all-reduce.1 = bf16[8,192,192]{2,1,0:T(8,128)(2,1)} all-reduce(f32[8,192,192]{2,1,0:T(8,128)} %reshape.31), channel_id=1, replica_groups=mesh['gx'=2,'gy'=4,'gz'=4] {'gz'}, use_global_device_ids=true, to_apply=%region_2.3 | all-reduce | flops 294912 | bytes 1769472 | tf_op jit(solution)/shard_map/psum | solution.py:46
  239.6 2.6 convolution_convert_fusion
  242.2 0.0 all-gather.3.cloned.1.call-update
  242.2 0.1 copy.24
  242.3 0.1 reshape.36
  242.4 6.3 %reshape.27 = bf16[32,192,192]{2,1,0:T(8,128)(2,1)} reshape(bf16[32,36864]{1,0:T(8,128)(2,1)} %param.10) | data formatting | bytes 4718592 | tf_op jit(solution)/shard_map/reshape | solution.py:16
  248.7 53.7 %all-gather.5.cloned.1.call-done = bf16[64,192,192]{2,1,0:T(8,128)(2,1)} async-done(((bf16[8,192,192]{2,1,0:T(8,128)(2,1)}), bf16[64,192,192]{2,1,0:T(8,128)(2,1)}) %all-gather.5.cloned.1.call-update) | async-done | bytes 4718608 | tf_op jit(solution)/shard_map/all_gather | solution.py:55
  302.4 6.3 %gather_fusion.1 = bf16[64,192,192]{2,1,0:T(8,128)(2,1)} fusion(bf16[64,192,192]{2,1,0:T(8,128)(2,1)} %all-gather.5.cloned.1.call-done, s32[1024]{0:T(1024)S(1)} %pad_clamp_fusion), kind=kCustom, calls=%fused_computation.1 | custom fusion | bytes 9437440 | tf_op jit(solution)/shard_map/gather | solution.py:57
  308.7 92.7 %all-gather.3.cloned.1.call-done = bf16[64,192,192]{2,1,0:T(8,128)(2,1)} async-done(((bf16[8,192,192]{2,1,0:T(8,128)(2,1)}), bf16[64,192,192]{2,1,0:T(8,128)(2,1)}) %all-gather.3.cloned.1.call-update) | async-done | bytes 4718608 | tf_op jit(solution)/shard_map/all_gather | solution.py:54
  401.4 6.4 %gather_fusion = bf16[64,192,192]{2,1,0:T(8,128)(2,1)} fusion(bf16[64,192,192]{2,1,0:T(8,128)(2,1)} %all-gather.3.cloned.1.call-done, s32[1024]{0:T(1024)S(1)} %pad_clamp_fusion), kind=kCustom, calls=%fused_computation | custom fusion | bytes 9437440 | tf_op jit(solution)/shard_map/gather | solution.py:58
  407.9 9.7 %copy.25 = f32[64,192,192]{1,2,0:T(8,128)} copy(bf16[64,192,192]{2,1,0:T(8,128)(2,1)} %gather_fusion) | data formatting | bytes 14155776 | tf_op jit(solution)/shard_map/convert_element_type | solution.py:62
  417.5 11.3 %fusion = bf16[32,2,192,192]{2,3,1,0:T(8,128)(2,1)} fusion(f32[32,2,192,192]{2,3,1,0:T(8,128)} %bitcast.27, bf16[32,2,192,192]{3,2,1,0:T(8,128)(2,1)} %bitcast.28, bf16[32,192,192]{2,1,0:T(8,128)(2,1)} %fusion.19), kind=kOutput, calls=%fused_computation.3 | convolution fusion | flops 915406848 | bytes 21233664 | tf_op jit(solution)/shard_map/pab,pebc->peac/dot_general | solution.py:59
  428.8 7.5 %fusion.9 = f32[32,192,192]{2,1,0:T(8,128)} fusion(bf16[32,192,192]{2,1,0:T(8,128)(2,1)S(1)} %reshape.29, bf16[32,2,192,192]{2,3,1,0:T(8,128)(2,1)} %fusion), kind=kOutput, calls=%fused_computation.15 | convolution fusion | flops 911867904 | bytes 15728640 | tf_op jit(solution)/shard_map/pab,pbc->pac/dot_general | solution.py:71
  436.3 7.9 %select_convert_fusion = bf16[32,192,192]{2,1,0:T(8,128)(2,1)S(1)} fusion(f32[32,192,192]{2,1,0:T(8,128)} %fusion.9, bf16[32,192,192]{2,1,0:T(8,128)(2,1)} %reshape.27, s32[32]{0:T(128)S(1)} %add_multiply_fusion, bf16[32,192,192]{2,1,0:T(8,128)(2,1)} %reshape.28), kind=kOutput, calls=%fused_computation.4 | convolution fusion | flops 467140608 | bytes 11796608 | tf_op jit(solution)/shard_map/pab,pbc->pac/dot_general | solution.py:34
  444.1 4.2 reshape.33
  (3 shorter events, 0.0 us)
Async XLA Ops:
  6.5 195.9 %reduce-scatter.2.cloned.1.call-start = ((), (), s32[]{:S(2)}) async-start(), calls=%async_computation.1 | async-start | bytes 10616832 | tf_op jit(solution)/shard_map/reduce_scatter | solution.py:40
  12.7 5.0 %copy-start.1 = (s32[32]{0:T(128)S(1)}, s32[32]{0:T(128)}, u32[]{:S(2)}) copy-start(s32[32]{0:T(128)} %param.7) | copy-start | bytes 388
  24.5 6.2 %copy-start = (s32[32,2]{0,1:T(2,128)S(1)}, s32[32,2]{0,1:T(2,128)}, u32[]{:S(2)}) copy-start(s32[32,2]{0,1:T(2,128)} %param.6) | copy-start | bytes 772
  37.5 264.9 %all-gather.5.cloned.1.call-start = ((), (), s32[]{:S(2)}) async-start(), calls=%async_computation.3 | async-start | bytes 7077888 | tf_op jit(solution)/shard_map/all_gather | solution.py:55
  40.5 361.0 %all-gather.3.cloned.1.call-start = ((), (), s32[]{:S(2)}) async-start(), calls=%async_computation.2 | async-start | bytes 7077888 | tf_op jit(solution)/shard_map/all_gather | solution.py:54
Sparse Core Ops, SparseCore 0:
  37.6 164.8 reduce-scatter.1
  204.6 97.7 all-gather.4
  304.5 96.8 all-gather.2
where the time goes:
time: 456 us; the launch traced here: 455 us
  waiting for transfers between devices  308 us (68%)
  local copies, waits for them, and re-layouts  56.5 us (12%)
  matrix products  42.8 us (9%)
  blocking collectives  34 us (7%)
  between operations  13.2 us (3%)
    reduce_scatter x1, waiting for transfers between devices, body(): lax.psum_scatter(jnp.dot(end_counts, flat_projected, preferred_element_ty...  162 us
    all_gather x1, waiting for transfers between devices, body(): lax.all_gather(coupled, ('gx', 'gy'), axis=0, tiled=True)  92.7 us
    all_gather x1, waiting for transfers between devices, body(): lax.all_gather(exchange_blocks, ('gx', 'gy'), axis=0, tiled=True)  53.7 us
    psum x1, blocking collectives, body(): domain = lax.psum(partial_sum, 'gz')  34 us
    dot_general x1, matrix products, body(): jnp.einsum('pab,pebc->peac', projected, picked_blocks, preferred_element_...  11.3 us
    convert_element_type x1, local copies, waits for them, and re-layouts, body(): picked_coupled.astype(jnp.float32) - own_term.astype(jnp.float32)  9.66 us
  transfers between devices with their start and end apart: 3, of which 3 were waited for; matrix products, arithmetic and copies ran while one was open for 5% of the time, Pallas kernels for 0%

commit v1 on v0

--- a/solution.py
+++ b/solution.py
@@ -43,7 +43,8 @@
         scatter_dimension=0,
         tiled=True,
     ).reshape(owned_rows, rank_width, rank_width)
-    domain = lax.psum(partial_sum, "gz")
+    parts = lax.all_gather(partial_sum, "gz", axis=0, tiled=False)
+    domain = parts.sum(axis=0)
     coupled = jnp.einsum(
         "oab,obc->oac",
         domain.astype(jnp.bfloat16),

time: 456 us -> 505 us (1.11)
  waiting for transfers between devices: 308 us -> 387 us
  blocking collectives: 34 us -> 0 us
    all_gather x0 -> x1, waiting for transfers between devices: none -> 42.4 us  [body(): parts = lax.all_gather(partial_sum, 'gz', axis=0, tiled=False)]
    psum x1 -> x0, blocking collectives: 34 us -> none  [body(): domain = lax.psum(partial_sum, 'gz')]
    all_gather x1, waiting for transfers between devices: 53.7 us -> 87.3 us  [body(): lax.all_gather(exchange_blocks, ('gx', 'gy'), axis=0, tiled=True)]
  transfers between devices with their start and end apart: 3 -> 4, of which waited for: 3 -> 4; matrix products, arithmetic and copies ran while one was open for 5% -> 5% of each run, Pallas kernels for 0% -> 0%
where the time goes in v1:
time: 505 us; the launch traced here: 504 us
  waiting for transfers between devices  387 us (77%)
  local copies, waits for them, and re-layouts  56.2 us (11%)
  matrix products  42.8 us (8%)
  between operations  13.2 us (3%)
    reduce_scatter x1, waiting for transfers between devices, body(): lax.psum_scatter(jnp.dot(end_counts, flat_projected, preferred_element_ty...  165 us
    all_gather x1, waiting for transfers between devices, body(): lax.all_gather(coupled, ('gx', 'gy'), axis=0, tiled=True)  92.5 us
    all_gather x1, waiting for transfers between devices, body(): lax.all_gather(exchange_blocks, ('gx', 'gy'), axis=0, tiled=True)  87.3 us
    all_gather x1, waiting for transfers between devices, body(): parts = lax.all_gather(partial_sum, 'gz', axis=0, tiled=False)  42.4 us
    dot_general x1, matrix products, body(): jnp.einsum('pab,pebc->peac', projected, picked_blocks, preferred_element_...  11.2 us
  transfers between devices with their start and end apart: 4, of which 4 were waited for; matrix products, arithmetic and copies ran while one was open for 5% of the time, Pallas kernels for 0%

profile of v1, /device:TPU:0, one launch (start us, length us, event | category | flops | bytes accessed | tf_op | source)
XLA Modules:
  0.0 504.3 jit_solution(6994494798054121088)
XLA Ops:
  6.5 0.0 reduce-scatter.2.cloned.1.call-start
  6.5 6.1 %reshape.25 = bf16[32,192,192]{2,1,0:T(8,128)(2,1)} reshape(bf16[32,36864]{1,0:T(8,128)(2,1)} %param.8) | data formatting | bytes 4718592 | tf_op jit(solution)/shard_map/reshape | solution.py:14
  12.6 0.0 copy-start.1
  12.6 5.0 reshape.26
  17.6 0.0 copy-done.1
  17.6 6.9 %fusion.19 = bf16[32,192,192]{2,1,0:T(8,128)(2,1)} fusion(bf16[32,192,192]{2,1,0:T(8,128)(2,1)S(1)} %reshape.26, bf16[32,192,192]{2,1,0:T(8,128)(2,1)} %reshape.25, s32[32]{0:T(128)S(1)} %add_multiply_fusion), kind=kOutput, calls=%fused_computation.20 | convolution fusion | flops 913047552 | bytes 7078016 | tf_op jit(solution)/shard_map/pab,pcb->pac/dot_general | solution.py:31
  24.6 0.0 copy-start
  24.6 6.2 %reshape.27 = bf16[32,36864]{1,0:T(8,128)(2,1)} reshape(bf16[32,192,192]{2,1,0:T(8,128)(2,1)} %fusion.19) | data formatting | bytes 4718592 | tf_op jit(solution)/shard_map/reshape | solution.py:35
  30.7 0.0 copy-done
  30.7 0.1 convert_reduce_fusion
  30.8 6.7 %fusion.26 = f32[64,36864]{1,0:T(8,128)} fusion(bf16[32,36864]{1,0:T(8,128)(2,1)} %reshape.27, s32[64,32]{0,1:T(8,128)S(1)} %convert_reduce_fusion), kind=kOutput, calls=%fused_computation.25 | convolution fusion | flops 150996992 | bytes 11804672 | tf_op jit(solution)/shard_map/dot_general | solution.py:41
  37.5 0.0 reduce-scatter.2.cloned.1.call-update
  37.5 0.0 all-gather.4.cloned.1.call-start
  37.6 164.9 %reduce-scatter.2.cloned.1.call-done = f32[8,36864]{1,0:T(8,128)} async-done(((f32[64,36864]{1,0:T(8,128)}), f32[8,36864]{1,0:T(8,128)}) %reduce-scatter.2.cloned.1.call-update) | async-done | bytes 1179664 | tf_op jit(solution)/shard_map/reduce_scatter | solution.py:40
  202.5 3.1 all_gather_reshape.3
  205.7 0.0 all-gather.4.cloned.1.call-update
  205.7 0.0 all-gather.8.cloned.1.call-start
  205.7 2.9 reshape.28
  208.6 0.0 all-gather.8.cloned.1.call-update
  208.7 0.2 all-gather.6.cloned.1.call-start
  208.9 42.4 %all-gather.4.cloned.1.call-done = f32[4,8,192,192]{3,2,1,0:T(8,128)} async-done(((f32[1,8,192,192]{3,2,1,0:T(8,128)}), f32[4,8,192,192]{3,2,1,0:T(8,128)}) %all-gather.4.cloned.1.call-update) | async-done | bytes 4718608 | tf_op jit(solution)/shard_map/all_gather | solution.py:46
  251.3 4.5 reduce_sum.19
  255.8 2.6 convolution_convert_fusion
  258.4 0.0 all-gather.6.cloned.1.call-update
  258.4 0.1 copy.24
  258.5 0.1 reshape.32
  258.6 6.1 %reshape.24 = bf16[32,192,192]{2,1,0:T(8,128)(2,1)} reshape(bf16[32,36864]{1,0:T(8,128)(2,1)} %param.10) | data formatting | bytes 4718592 | tf_op jit(solution)/shard_map/reshape | solution.py:16
  264.8 87.3 %all-gather.8.cloned.1.call-done = bf16[64,192,192]{2,1,0:T(8,128)(2,1)} async-done(((bf16[8,192,192]{2,1,0:T(8,128)(2,1)}), bf16[64,192,192]{2,1,0:T(8,128)(2,1)}) %all-gather.8.cloned.1.call-update) | async-done | bytes 4718608 | tf_op jit(solution)/shard_map/all_gather | solution.py:56
  352.1 6.3 %gather_fusion.1 = bf16[64,192,192]{2,1,0:T(8,128)(2,1)} fusion(bf16[64,192,192]{2,1,0:T(8,128)(2,1)} %all-gather.8.cloned.1.call-done, s32[1024]{0:T(1024)S(1)} %pad_clamp_fusion), kind=kCustom, calls=%fused_computation.1 | custom fusion | bytes 9437440 | tf_op jit(solution)/shard_map/gather | solution.py:58
  358.4 92.5 %all-gather.6.cloned.1.call-done = bf16[64,192,192]{2,1,0:T(8,128)(2,1)} async-done(((bf16[8,192,192]{2,1,0:T(8,128)(2,1)}), bf16[64,192,192]{2,1,0:T(8,128)(2,1)}) %all-gather.6.cloned.1.call-update) | async-done | bytes 4718608 | tf_op jit(solution)/shard_map/all_gather | solution.py:55
  451.0 6.3 %gather_fusion = bf16[64,192,192]{2,1,0:T(8,128)(2,1)} fusion(bf16[64,192,192]{2,1,0:T(8,128)(2,1)} %all-gather.6.cloned.1.call-done, s32[1024]{0:T(1024)S(1)} %pad_clamp_fusion), kind=kCustom, calls=%fused_computation | custom fusion | bytes 9437440 | tf_op jit(solution)/shard_map/gather | solution.py:59
  457.3 9.7 %copy.25 = f32[64,192,192]{1,2,0:T(8,128)} copy(bf16[64,192,192]{2,1,0:T(8,128)(2,1)} %gather_fusion) | data formatting | bytes 14155776 | tf_op jit(solution)/shard_map/convert_element_type | solution.py:63
  467.0 11.2 %fusion = bf16[32,2,192,192]{2,3,1,0:T(8,128)(2,1)} fusion(f32[32,2,192,192]{2,3,1,0:T(8,128)} %bitcast.27, bf16[32,2,192,192]{3,2,1,0:T(8,128)(2,1)} %bitcast.28, bf16[32,192,192]{2,1,0:T(8,128)(2,1)} %fusion.19), kind=kOutput, calls=%fused_computation.3 | convolution fusion | flops 915406848 | bytes 21233664 | tf_op jit(solution)/shard_map/pab,pebc->peac/dot_general | solution.py:60
  478.2 7.5 %fusion.9 = f32[32,192,192]{2,1,0:T(8,128)} fusion(bf16[32,192,192]{2,1,0:T(8,128)(2,1)S(1)} %reshape.26, bf16[32,2,192,192]{2,3,1,0:T(8,128)(2,1)} %fusion), kind=kOutput, calls=%fused_computation.15 | convolution fusion | flops 911867904 | bytes 15728640 | tf_op jit(solution)/shard_map/pab,pbc->pac/dot_general | solution.py:72
  485.7 7.9 %select_convert_fusion = bf16[32,192,192]{2,1,0:T(8,128)(2,1)S(1)} fusion(f32[32,192,192]{2,1,0:T(8,128)} %fusion.9, bf16[32,192,192]{2,1,0:T(8,128)(2,1)} %reshape.24, s32[32]{0:T(128)S(1)} %add_multiply_fusion, bf16[32,192,192]{2,1,0:T(8,128)(2,1)} %reshape.25), kind=kOutput, calls=%fused_computation.4 | convolution fusion | flops 467140608 | bytes 11796608 | tf_op jit(solution)/shard_map/pab,pbc->pac/dot_general | solution.py:34
  493.6 4.2 reshape.29
  (3 shorter events, 0.0 us)
Async XLA Ops:
  6.5 196.0 %reduce-scatter.2.cloned.1.call-start = ((), (), s32[]{:S(2)}) async-start(), calls=%async_computation.1 | async-start | bytes 10616832 | tf_op jit(solution)/shard_map/reduce_scatter | solution.py:40
  12.6 5.0 copy-start.1
  24.6 6.2 %copy-start = (s32[32,2]{0,1:T(2,128)S(1)}, s32[32,2]{0,1:T(2,128)}, u32[]{:S(2)}) copy-start(s32[32,2]{0,1:T(2,128)} %param.6) | copy-start | bytes 772
  37.5 213.7 %all-gather.4.cloned.1.call-start = ((), (), s32[]{:S(2)}) async-start(), calls=%async_computation.2 | async-start | bytes 7864320 | tf_op jit(solution)/shard_map/all_gather | solution.py:46
  205.7 146.4 %all-gather.8.cloned.1.call-start = ((), (), s32[]{:S(2)}) async-start(), calls=%async_computation.4 | async-start | bytes 7077888 | tf_op jit(solution)/shard_map/all_gather | solution.py:56
  208.7 242.3 %all-gather.6.cloned.1.call-start = ((), (), s32[]{:S(2)}) async-start(), calls=%async_computation.3 | async-start | bytes 7077888 | tf_op jit(solution)/shard_map/all_gather | solution.py:55
Sparse Core Ops, SparseCore 0:
  37.7 164.8 reduce-scatter.1
  205.8 45.4 all-gather.3
  253.4 98.6 all-gather.7
  354.1 96.8 all-gather.5
